TPU v7x, 32 devices: a whole 2x2x4 slice. The times are simulated.
32 devices in a mesh: gx: 8 (over y, x, core), gy: 4 (over z).
Axes of the slice: x: 2, y: 2, z: 4, core: 2. Of those that a mesh axis runs over, the one named last changes fastest.
Arguments:
- field: float32 [65536, 512], P(('gx', 'gy')), may hold values from -6 to 6
Outputs:
- spectrum: float32 [65536, 512], P('gx', 'gy')
All inputs are finite; a program needn't handle non-finite values.
Results may differ from a plain program's by a relative error of at most 0.00007.
Values sent between devices are 32-bit elements; how exact they have to be, the bound alone decides.
A program may use at most 64 MiB of HBM per device.

v0:
```python
import math
import jax
import jax.numpy as jnp
from jax import lax
from jax.sharding import PartitionSpec as P

P_SIZE = 256
Q = 256
highest = lax.Precision.HIGHEST


def mat_dot(left, right):
    return jnp.dot(left, right, precision=highest, preferred_element_type=jnp.float32)


def finish(spec_real, spec_imag, frequency):
    length = P_SIZE * Q
    phases = math.pi / (2.0 * length) * frequency.astype(jnp.float32)
    factor = math.sqrt(2.0 / length)
    return factor * (
        jnp.cos(phases)[:, :, None] * spec_real + jnp.sin(phases)[:, :, None] * spec_imag
    )


def body(field):
    groups = lax.axis_size("gx")
    position = lax.axis_index("gx")
    length = P_SIZE * Q
    joined = lax.all_to_all(field, "gy", split_axis=1, concat_axis=0, tiled=True)
    row_count = joined.shape[0]
    col_width = joined.shape[1]
    half_rows = P_SIZE // (2 * groups)
    local_q = Q // groups
    local_p = P_SIZE // groups
    paired = joined.reshape(row_count // 2, 2, col_width)
    even_rows = paired[:, 0].reshape(half_rows, Q, col_width)
    odd_rows = jnp.flip(paired[:, 1].reshape(half_rows, Q, col_width), axis=1)
    low_half, high_half = (
        lax.all_to_all(even_rows, "gx", split_axis=1, concat_axis=0, tiled=True),
        lax.all_to_all(odd_rows, "gx", split_axis=1, concat_axis=0, tiled=True),
    )
    freq_first = jnp.arange(P_SIZE, dtype=jnp.int32)
    place_low = jnp.arange(P_SIZE // 2, dtype=jnp.int32)
    place_high = P_SIZE - 1 - place_low
    two_pi = 2.0 * math.pi
    low_phase = (
        two_pi / P_SIZE * (freq_first[:, None] * place_low[None, :] % P_SIZE).astype(jnp.float32)
    )
    high_phase = (
        two_pi / P_SIZE * (freq_first[:, None] * place_high[None, :] % P_SIZE).astype(jnp.float32)
    )
    flat_low = low_half.reshape(P_SIZE // 2, local_q * col_width)
    flat_high = high_half.reshape(P_SIZE // 2, local_q * col_width)
    cos_part = (
        mat_dot(jnp.cos(low_phase), flat_low) + mat_dot(jnp.cos(high_phase), flat_high)
    ).reshape(P_SIZE, local_q, col_width)
    sin_part = (
        mat_dot(jnp.sin(low_phase), flat_low) + mat_dot(jnp.sin(high_phase), flat_high)
    ).reshape(P_SIZE, local_q, col_width)
    part_imag = -sin_part
    second_place = position * local_q + jnp.arange(local_q, dtype=jnp.int32)
    turn_phase = (
        two_pi / length * (freq_first[:, None] * second_place[None, :] % length).astype(jnp.float32)
    )
    turn_cos = jnp.cos(turn_phase)[:, :, None]
    turn_sin = jnp.sin(turn_phase)[:, :, None]
    turned_real = cos_part * turn_cos + part_imag * turn_sin
    turned_imag = part_imag * turn_cos - cos_part * turn_sin
    moved_real, moved_imag = (
        lax.all_to_all(turned_real, "gx", split_axis=0, concat_axis=1, tiled=True),
        lax.all_to_all(turned_imag, "gx", split_axis=0, concat_axis=1, tiled=True),
    )
    second_index = jnp.arange(Q, dtype=jnp.int32)
    row_phase = two_pi / Q * (second_index[:, None] * second_index[None, :] % Q).astype(jnp.float32)
    row_cos = jnp.cos(row_phase)
    row_sin = jnp.sin(row_phase)
    spec_real = jnp.einsum("jb,kbc->jkc", row_cos, moved_real, precision=highest) + jnp.einsum(
        "jb,kbc->jkc", row_sin, moved_imag, precision=highest
    )
    spec_imag = jnp.einsum("jb,kbc->jkc", row_cos, moved_imag, precision=highest) - jnp.einsum(
        "jb,kbc->jkc", row_sin, moved_real, precision=highest
    )
    block_rows = lax.dynamic_slice_in_dim(freq_first, position * local_p, local_p, 0)
    frequency = block_rows[None, :] + P_SIZE * second_index[:, None]
    result = finish(spec_real, spec_imag, frequency)
    arrived = lax.all_to_all(result, "gx", split_axis=0, concat_axis=1, tiled=True)
    return arrived.reshape(local_q * P_SIZE, col_width)


def solution(mesh):
    in_specs = (P(("gx", "gy"), None),)
    out_specs = P("gx", "gy")
    return jax.shard_map(body, mesh=mesh, in_specs=in_specs, out_specs=out_specs, check_vma=False)
```

profile of v0, /device:TPU:0, one launch (start us, length us, event | category | flops | bytes accessed | tf_op | source)
XLA Modules:
  0.0 380.9 jit_solution(13258083812697321297)
XLA Ops:
  0.0 5.3 %copy.15 = f32[2048,512]{0,1:T(8,128)} copy(f32[2048,512]{1,0:T(8,128)} %param.1) | data formatting | bytes 8388608 | tf_op args[0]
  5.3 100.6 %all_to_all.97 = f32[2048,4,128]{0,2,1:T(8,128)} all-to-all(f32[2048,4,128]{0,2,1:T(8,128)} %bitcast.81), channel_id=1, replica_groups=mesh['gx'=8,'gy'=4] {'gy'}, dimensions={1} | all-to-all | bytes 8388608 | tf_op jit(solution)/shard_map/all_to_all | solution.py:29
  105.9 5.3 %copy.16 = f32[4,2048,128]{2,1,0:T(8,128)} copy(f32[4,2048,128]{1,2,0:T(8,128)} %bitcast.79) | data formatting | bytes 8388608 | tf_op jit(solution)/shard_map/all_to_all | solution.py:29
  111.2 7.7 %fusion.96 = (f32[4096,1,128]{2,1,0:T(1,128)}, f32[4096,1,128]{2,1,0:T(1,128)S(1)}) fusion(f32[4096,2,128]{2,1,0:T(2,128)} %bitcast.78), kind=kLoop, calls=%fused_computation.111 | loop fusion | bytes 8388608 | tf_op jit(solution)/shard_map/slice | solution.py:37
  118.9 2.5 copy.17
  121.4 3.8 all-to-all-start.1
  125.2 4.1 %copy.20 = f32[16,256,128]{2,0,1:T(8,128)} copy(f32[16,256,128]{2,1,0:T(8,128)} %bitcast.83) | data formatting | bytes 4194304 | tf_op jit(solution)/shard_map/reshape;squeeze | solution.py:37
  129.3 3.1 rev.4
  132.4 19.4 %all-to-all-done.1 = f32[16,256,128]{2,0,1:T(8,128)S(1)} async-done(((f32[16,256,128]{2,0,1:T(8,128)}), f32[16,256,128]{2,0,1:T(8,128)S(1)}, u32[]{:S(2)}, u32[]{:S(2)}) %all-to-all-start.1) | async-done | bytes 2097184 | tf_op jit(solution)/shard_map/all_to_all | solution.py:39
  151.8 4.9 %all-to-all-start.2 = ((f32[16,256,128]{2,0,1:T(8,128)}), f32[16,256,128]{2,0,1:T(8,128)}, u32[]{:S(2)}, u32[]{:S(2)}) async-start(f32[16,256,128]{2,0,1:T(8,128)} %rev.4), calls=%async_computation.2 | async-start | bytes 4194304 | tf_op jit(solution)/shard_map/all_to_all | solution.py:40
  157.9 7.3 %fusion.9 = f32[256,4096]{1,0:T(8,128)} fusion(f32[16,8,32,128]{3,2,1,0:T(8,128)S(1)} %bitcast.73), kind=kOutput, calls=%fused_computation.16 | convolution fusion | flops 1611071488 | bytes 6291456 | tf_op jit(solution)/shard_map/dot_general | solution.py:13
  165.2 7.5 %fusion.7 = f32[256,4096]{1,0:T(8,128)} fusion(f32[16,8,32,128]{3,2,1,0:T(8,128)S(1)} %bitcast.74), kind=kOutput, calls=%fused_computation.14 | convolution fusion | flops 1611071488 | bytes 6291456 | tf_op jit(solution)/shard_map/dot_general | solution.py:13
  172.7 10.6 %all-to-all-done.2 = f32[16,256,128]{2,0,1:T(8,128)} async-done(((f32[16,256,128]{2,0,1:T(8,128)}), f32[16,256,128]{2,0,1:T(8,128)}, u32[]{:S(2)}, u32[]{:S(2)}) %all-to-all-start.2) | async-done | bytes 2097184 | tf_op jit(solution)/shard_map/all_to_all | solution.py:40
  183.3 2.4 copy.22
  186.1 4.9 %fusion.3 = f32[32,8,32,128]{3,1,2,0:T(8,128)S(1)} fusion(f32[256,4096]{1,0:T(8,128)S(1)} %copy-done.3, f32[16,8,32,128]{3,2,1,0:T(8,128)S(1)} %bitcast.75, s32[128]{0:T(128)S(1)} %iota_subtract_fusion), kind=kOutput, calls=%fused_computation.10 | convolution fusion | flops 1612120064 | bytes 10486272 | tf_op jit(solution)/shard_map/dot_general | solution.py:13
  191.1 0.8 copy.31
  191.9 1.4 copy-done.2
  193.3 5.0 %fusion.4 = f32[32,8,32,128]{3,1,2,0:T(8,128)S(1)} fusion(f32[256,4096]{1,0:T(8,128)S(1)} %copy-done.2, f32[16,8,32,128]{3,2,1,0:T(8,128)S(1)} %bitcast.76, s32[128]{0:T(128)S(1)} %iota_subtract_fusion), kind=kOutput, calls=%fused_computation.11 | convolution fusion | flops 1613168640 | bytes 10486272 | tf_op jit(solution)/shard_map/dot_general | solution.py:13
  198.2 1.0 copy.32
  199.2 4.6 %fusion.1 = (f32[256,32,128]{2,1,0:T(8,128)}, f32[256,32,128]{2,1,0:T(8,128)S(1)}) fusion(f32[32,8,32,128]{3,2,1,0:T(8,128)S(1)} %copy.32, f32[32,8,32,128]{3,2,1,0:T(8,128)S(1)} %copy.31, f32[256,32]{1,0:T(8,128)S(1)} %get-tuple-element.12, f32[256,32]{1,0:T(8,128)S(1)} %get-tuple-element.11), kind=kLoop, calls=%fused_computation.5 | loop fusion | flops 6291456 | bytes 16842752 | tf_op jit(solution)/shard_map/add | solution.py:67
  203.8 52.3 %all_to_all.98 = f32[256,32,128]{2,1,0:T(8,128)} all-to-all(f32[256,32,128]{2,1,0:T(8,128)S(1)} %get-tuple-element.6), channel_id=1, replica_groups=mesh['gx'=8,'gy'=4] {'gx'}, dimensions={0} | all-to-all | bytes 8388608 | tf_op jit(solution)/shard_map/all_to_all | solution.py:71
  256.1 4.6 %all-to-all-start.3 = ((f32[256,32,128]{2,1,0:T(8,128)}), f32[256,32,128]{2,1,0:T(8,128)}, u32[]{:S(2)}, u32[]{:S(2)}) async-start(f32[256,32,128]{2,1,0:T(8,128)} %get-tuple-element.5), calls=%async_computation.3 | async-start | bytes 8388608 | tf_op jit(solution)/shard_map/all_to_all | solution.py:70
  261.0 2.8 copy.24
  263.8 7.1 %fusion.19 = f32[256,32,128]{2,0,1:T(8,128)} fusion(f32[32,256,128]{2,1,0:T(8,128)S(1)} %bitcast.71), kind=kOutput, calls=%fused_computation.29 | convolution fusion | flops 3222142976 | bytes 8388608 | tf_op jit(solution)/shard_map/jb,kbc->jkc/dot_general | solution.py:77
  270.9 7.3 %fusion.21 = f32[256,32,128]{2,0,1:T(8,128)} fusion(f32[32,256,128]{2,1,0:T(8,128)S(1)} %bitcast.72), kind=kOutput, calls=%fused_computation.31 | convolution fusion | flops 3222142976 | bytes 8388608 | tf_op jit(solution)/shard_map/jb,kbc->jkc/dot_general | solution.py:80
  278.2 31.5 %all-to-all-done.3 = f32[256,32,128]{2,1,0:T(8,128)} async-done(((f32[256,32,128]{2,1,0:T(8,128)}), f32[256,32,128]{2,1,0:T(8,128)}, u32[]{:S(2)}, u32[]{:S(2)}) %all-to-all-start.3) | async-done | bytes 4194336 | tf_op jit(solution)/shard_map/all_to_all | solution.py:70
  309.8 2.8 copy.23
  312.6 4.8 %fusion.23 = f32[256,32,128]{2,0,1:T(8,128)S(1)} fusion(f32[32,256,128]{2,1,0:T(8,128)S(1)} %bitcast.69), kind=kOutput, calls=%fused_computation.33 | convolution fusion | flops 3222142976 | bytes 8388608 | tf_op jit(solution)/shard_map/jb,kbc->jkc/dot_general | solution.py:77
  317.4 6.1 %add_multiply_fusion = f32[256,32,128]{2,0,1:T(8,128)S(1)} fusion(f32[256,32,128]{2,0,1:T(8,128)S(1)} %copy-done.1, f32[256,32,128]{2,0,1:T(8,128)S(1)} %fusion.23, f32[256,32,128]{2,0,1:T(8,128)S(1)} %copy-done, f32[32,256,128]{2,1,0:T(8,128)S(1)} %bitcast.70, f32[256,32]{0,1:T(8,128)S(1)} %get-tuple-element.10, f32[256,32]{0,1:T(8,128)S(1)} %get-tuple-element.9), kind=kOutput, calls=%fused_computation.9 | convolution fusion | flops 3228434432 | bytes 21037056 | tf_op jit(solution)/shard_map/jb,kbc->jkc/dot_general | solution.py:80
  323.5 2.7 copy.25
  326.3 51.5 %all_to_all.99 = f32[256,32,128]{2,1,0:T(8,128)S(1)} all-to-all(f32[256,32,128]{2,1,0:T(8,128)S(1)} %copy.25), channel_id=1, replica_groups=mesh['gx'=8,'gy'=4] {'gx'}, dimensions={0} | all-to-all | bytes 8388608 | tf_op jit(solution)/shard_map/all_to_all | solution.py:86
  377.8 2.7 copy.26
  (15 shorter events, 1.9 us)
Async XLA Ops:
  121.4 30.4 %all-to-all-start.1 = ((f32[16,256,128]{2,0,1:T(8,128)}), f32[16,256,128]{2,0,1:T(8,128)S(1)}, u32[]{:S(2)}, u32[]{:S(2)}) async-start(f32[16,256,128]{2,0,1:T(8,128)} %copy.17), calls=%async_computation.1 | async-start | bytes 4194304 | tf_op jit(solution)/shard_map/all_to_all | solution.py:39
  151.8 31.5 %all-to-all-start.2 = ((f32[16,256,128]{2,0,1:T(8,128)}), f32[16,256,128]{2,0,1:T(8,128)}, u32[]{:S(2)}, u32[]{:S(2)}) async-start(f32[16,256,128]{2,0,1:T(8,128)} %rev.4), calls=%async_computation.2 | async-start | bytes 4194304 | tf_op jit(solution)/shard_map/all_to_all | solution.py:40
  183.3 2.8 copy-start.3
  191.1 2.2 copy-start.2
  256.1 53.7 %all-to-all-start.3 = ((f32[256,32,128]{2,1,0:T(8,128)}), f32[256,32,128]{2,1,0:T(8,128)}, u32[]{:S(2)}, u32[]{:S(2)}) async-start(f32[256,32,128]{2,1,0:T(8,128)} %get-tuple-element.5), calls=%async_computation.3 | async-start | bytes 8388608 | tf_op jit(solution)/shard_map/all_to_all | solution.py:70
  312.6 4.8 %copy-start = (f32[256,32,128]{2,0,1:T(8,128)S(1)}, f32[256,32,128]{2,0,1:T(8,128)}, u32[]{:S(2)}) copy-start(f32[256,32,128]{2,0,1:T(8,128)} %fusion.19) | copy-start | bytes 12582916
  312.6 4.8 %copy-start.1 = (f32[256,32,128]{2,0,1:T(8,128)S(1)}, f32[256,32,128]{2,0,1:T(8,128)}, u32[]{:S(2)}) copy-start(f32[256,32,128]{2,0,1:T(8,128)} %fusion.21) | copy-start | bytes 12582916
where the time goes:
time: 386 us; the launch traced here: 381 us
  blocking collectives  204 us (53%)
  waiting for transfers between devices  61.6 us (16%)
  matrix products  50 us (13%)
  local copies, waits for them, and re-layouts  45.8 us (12%)
  starting transfers between devices  13.2 us (3%)
  other arithmetic  5.36 us (1%)
    all_to_all x1, blocking collectives, body(): lax.all_to_all(field, 'gy', split_axis=1, concat_axis=0, tiled=True)  101 us
    all_to_all x1, blocking collectives, body(): lax.all_to_all(turned_imag, 'gx', split_axis=0, concat_axis=1, tiled=True)  52.3 us
    all_to_all x1, blocking collectives, body(): lax.all_to_all(result, 'gx', split_axis=0, concat_axis=1, tiled=True)  51.5 us
    all_to_all x1, waiting for transfers between devices, body(): lax.all_to_all(turned_real, 'gx', split_axis=0, concat_axis=1, tiled=True)  31.5 us
    dot_general x4, matrix products, mat_dot(): jnp.dot(left, right, precision=highest, preferred_element_type=jnp.float32)  24.7 us
    all_to_all x1, waiting for transfers between devices, body(): lax.all_to_all(even_rows, 'gx', split_axis=1, concat_axis=0, tiled=True)  19.4 us
    all_to_all x1, waiting for transfers between devices, body(): lax.all_to_all(odd_rows, 'gx', split_axis=1, concat_axis=0, tiled=True)  10.6 us
    unnamed x11, local copies, waits for them, and re-layouts  8.93 us
  transfers between devices with their start and end apart: 3, of which 3 were waited for; matrix products, arithmetic and copies ran while one was open for 11% of the time, Pallas kernels for 0%

commit v1 on v0

--- a/solution.py
+++ b/solution.py
@@ -7,6 +7,13 @@
 P_SIZE = 256
 Q = 256
 highest = lax.Precision.HIGHEST
+
+
+def swap_blocks(x, mesh_axis, split, join):
+    size = lax.axis_size(mesh_axis)
+    blocks = jnp.stack(jnp.split(x, size, axis=split), axis=0)
+    blocks = lax.all_to_all(blocks, mesh_axis, split_axis=0, concat_axis=0)
+    return jnp.concatenate(blocks, axis=join)
 
 
 def mat_dot(left, right):
@@ -68,7 +75,7 @@
     turned_imag = part_imag * turn_cos - cos_part * turn_sin
     moved_real, moved_imag = (
         lax.all_to_all(turned_real, "gx", split_axis=0, concat_axis=1, tiled=True),
-        lax.all_to_all(turned_imag, "gx", split_axis=0, concat_axis=1, tiled=True),
+        swap_blocks(turned_imag, "gx", 0, 1),
     )
     second_index = jnp.arange(Q, dtype=jnp.int32)
     row_phase = two_pi / Q * (second_index[:, None] * second_index[None, :] % Q).astype(jnp.float32)

time: 386 us -> 386 us (level)
    unnamed x11 -> x18, local copies, waits for them, and re-layouts: 8.93 us -> 9.19 us
where the time goes in v1:
time: 386 us; the launch traced here: 381 us
  blocking collectives  204 us (53%)
  waiting for transfers between devices  61.6 us (16%)
  matrix products  50 us (13%)
  local copies, waits for them, and re-layouts  46.1 us (12%)
  starting transfers between devices  13.2 us (3%)
  other arithmetic  5.35 us (1%)
    all_to_all x1, blocking collectives, body(): lax.all_to_all(field, 'gy', split_axis=1, concat_axis=0, tiled=True)  101 us
    all_to_all x1, blocking collectives, swap_blocks(): blocks = lax.all_to_all(blocks, mesh_axis, split_axis=0, concat_axis=0)  52.3 us
    all_to_all x1, blocking collectives, body(): lax.all_to_all(result, 'gx', split_axis=0, concat_axis=1, tiled=True)  51.5 us
    all_to_all x1, waiting for transfers between devices, body(): lax.all_to_all(turned_real, 'gx', split_axis=0, concat_axis=1, tiled=True)  31.5 us
    dot_general x4, matrix products, mat_dot(): jnp.dot(left, right, precision=highest, preferred_element_type=jnp.float32)  24.7 us
    all_to_all x1, waiting for transfers between devices, body(): lax.all_to_all(even_rows, 'gx', split_axis=1, concat_axis=0, tiled=True)  19.4 us
    all_to_all x1, waiting for transfers between devices, body(): lax.all_to_all(odd_rows, 'gx', split_axis=1, concat_axis=0, tiled=True)  10.6 us
    unnamed x18, local copies, waits for them, and re-layouts  9.19 us
  transfers between devices with their start and end apart: 3, of which 3 were waited for; matrix products, arithmetic and copies ran while one was open for 11% of the time, Pallas kernels for 0%

profile of v1, /device:TPU:0, one launch (start us, length us, event | category | flops | bytes accessed | tf_op | source)
XLA Modules:
  0.0 381.3 jit_solution(16232786728314117846)
XLA Ops:
  0.0 5.3 %copy.15 = f32[2048,512]{0,1:T(8,128)} copy(f32[2048,512]{1,0:T(8,128)} %param.1) | data formatting | bytes 8388608 | tf_op args[0]
  5.3 100.6 %all_to_all.84 = f32[2048,4,128]{0,2,1:T(8,128)} all-to-all(f32[2048,4,128]{0,2,1:T(8,128)} %bitcast.111), channel_id=1, replica_groups=mesh['gx'=8,'gy'=4] {'gy'}, dimensions={1} | all-to-all | bytes 8388608 | tf_op jit(solution)/shard_map/all_to_all | solution.py:36
  105.9 5.3 %copy.16 = f32[4,2048,128]{2,1,0:T(8,128)} copy(f32[4,2048,128]{1,2,0:T(8,128)} %bitcast.109) | data formatting | bytes 8388608 | tf_op jit(solution)/shard_map/all_to_all | solution.py:36
  111.2 7.7 %fusion.104 = (f32[4096,1,128]{2,1,0:T(1,128)}, f32[4096,1,128]{2,1,0:T(1,128)S(1)}) fusion(f32[4096,2,128]{2,1,0:T(2,128)} %bitcast.108), kind=kLoop, calls=%fused_computation.127 | loop fusion | bytes 8388608 | tf_op jit(solution)/shard_map/slice | solution.py:44
  118.9 2.5 copy.17
  121.4 3.8 all-to-all-start.1
  125.2 4.1 %copy.20 = f32[16,256,128]{2,0,1:T(8,128)} copy(f32[16,256,128]{2,1,0:T(8,128)} %bitcast.113) | data formatting | bytes 4194304 | tf_op jit(solution)/shard_map/reshape;squeeze | solution.py:44
  129.3 3.1 rev.4
  132.4 19.4 %all-to-all-done.1 = f32[16,256,128]{2,0,1:T(8,128)S(1)} async-done(((f32[16,256,128]{2,0,1:T(8,128)}), f32[16,256,128]{2,0,1:T(8,128)S(1)}, u32[]{:S(2)}, u32[]{:S(2)}) %all-to-all-start.1) | async-done | bytes 2097184 | tf_op jit(solution)/shard_map/all_to_all | solution.py:46
  151.8 4.9 %all-to-all-start.2 = ((f32[16,256,128]{2,0,1:T(8,128)}), f32[16,256,128]{2,0,1:T(8,128)}, u32[]{:S(2)}, u32[]{:S(2)}) async-start(f32[16,256,128]{2,0,1:T(8,128)} %rev.4), calls=%async_computation.2 | async-start | bytes 4194304 | tf_op jit(solution)/shard_map/all_to_all | solution.py:47
  157.9 7.3 %fusion.9 = f32[256,4096]{1,0:T(8,128)} fusion(f32[16,8,32,128]{3,2,1,0:T(8,128)S(1)} %bitcast.103), kind=kOutput, calls=%fused_computation.16 | convolution fusion | flops 1611071488 | bytes 6291456 | tf_op jit(solution)/shard_map/dot_general | solution.py:20
  165.2 7.5 %fusion.7 = f32[256,4096]{1,0:T(8,128)} fusion(f32[16,8,32,128]{3,2,1,0:T(8,128)S(1)} %bitcast.104), kind=kOutput, calls=%fused_computation.14 | convolution fusion | flops 1611071488 | bytes 6291456 | tf_op jit(solution)/shard_map/dot_general | solution.py:20
  172.7 10.6 %all-to-all-done.2 = f32[16,256,128]{2,0,1:T(8,128)} async-done(((f32[16,256,128]{2,0,1:T(8,128)}), f32[16,256,128]{2,0,1:T(8,128)}, u32[]{:S(2)}, u32[]{:S(2)}) %all-to-all-start.2) | async-done | bytes 2097184 | tf_op jit(solution)/shard_map/all_to_all | solution.py:47
  183.3 2.4 copy.22
  186.1 4.9 %fusion.3 = f32[32,8,32,128]{3,1,2,0:T(8,128)S(1)} fusion(f32[256,4096]{1,0:T(8,128)S(1)} %copy-done.3, f32[16,8,32,128]{3,2,1,0:T(8,128)S(1)} %bitcast.105, s32[128]{0:T(128)S(1)} %iota_subtract_fusion), kind=kOutput, calls=%fused_computation.10 | convolution fusion | flops 1612120064 | bytes 10486272 | tf_op jit(solution)/shard_map/dot_general | solution.py:20
  191.1 0.8 copy.31
  191.9 1.4 copy-done.2
  193.3 5.0 %fusion.4 = f32[32,8,32,128]{3,1,2,0:T(8,128)S(1)} fusion(f32[256,4096]{1,0:T(8,128)S(1)} %copy-done.2, f32[16,8,32,128]{3,2,1,0:T(8,128)S(1)} %bitcast.106, s32[128]{0:T(128)S(1)} %iota_subtract_fusion), kind=kOutput, calls=%fused_computation.11 | convolution fusion | flops 1613168640 | bytes 10486272 | tf_op jit(solution)/shard_map/dot_general | solution.py:20
  198.2 1.0 copy.32
  199.2 4.6 %fusion.1 = (f32[256,32,128]{2,1,0:T(8,128)}, f32[256,32,128]{2,1,0:T(8,128)S(1)}) fusion(f32[32,8,32,128]{3,2,1,0:T(8,128)S(1)} %copy.32, f32[32,8,32,128]{3,2,1,0:T(8,128)S(1)} %copy.31, f32[256,32]{1,0:T(8,128)S(1)} %get-tuple-element.12, f32[256,32]{1,0:T(8,128)S(1)} %get-tuple-element.11), kind=kLoop, calls=%fused_computation.5 | loop fusion | flops 6291456 | bytes 16842752 | tf_op jit(solution)/shard_map/add | solution.py:74
  204.2 52.3 %all_to_all.85 = f32[8,32,32,128]{3,2,1,0:T(8,128)} all-to-all(f32[8,32,32,128]{3,2,1,0:T(8,128)S(1)} %fusion.15), channel_id=1, replica_groups=mesh['gx'=8,'gy'=4] {'gx'}, dimensions={0} | all-to-all | bytes 8388608 | tf_op jit(solution)/shard_map/all_to_all | solution.py:15
  256.5 4.6 %all-to-all-start.3 = ((f32[256,32,128]{2,1,0:T(8,128)}), f32[256,32,128]{2,1,0:T(8,128)}, u32[]{:S(2)}, u32[]{:S(2)}) async-start(f32[256,32,128]{2,1,0:T(8,128)} %get-tuple-element.5), calls=%async_computation.3 | async-start | bytes 8388608 | tf_op jit(solution)/shard_map/all_to_all | solution.py:77
  261.3 2.8 copy.24
  264.2 7.1 %fusion.27 = f32[256,32,128]{2,0,1:T(8,128)} fusion(f32[32,256,128]{2,1,0:T(8,128)S(1)} %bitcast.101), kind=kOutput, calls=%fused_computation.45 | convolution fusion | flops 3222142976 | bytes 8388608 | tf_op jit(solution)/shard_map/jb,kbc->jkc/dot_general | solution.py:84
  271.3 7.3 %fusion.29 = f32[256,32,128]{2,0,1:T(8,128)} fusion(f32[32,256,128]{2,1,0:T(8,128)S(1)} %bitcast.102), kind=kOutput, calls=%fused_computation.47 | convolution fusion | flops 3222142976 | bytes 8388608 | tf_op jit(solution)/shard_map/jb,kbc->jkc/dot_general | solution.py:87
  278.6 31.5 %all-to-all-done.3 = f32[256,32,128]{2,1,0:T(8,128)} async-done(((f32[256,32,128]{2,1,0:T(8,128)}), f32[256,32,128]{2,1,0:T(8,128)}, u32[]{:S(2)}, u32[]{:S(2)}) %all-to-all-start.3) | async-done | bytes 4194336 | tf_op jit(solution)/shard_map/all_to_all | solution.py:77
  310.1 2.8 copy.23
  313.0 4.8 %fusion.31 = f32[256,32,128]{2,0,1:T(8,128)S(1)} fusion(f32[32,256,128]{2,1,0:T(8,128)S(1)} %bitcast.99), kind=kOutput, calls=%fused_computation.49 | convolution fusion | flops 3222142976 | bytes 8388608 | tf_op jit(solution)/shard_map/jb,kbc->jkc/dot_general | solution.py:84
  317.8 6.1 %add_multiply_fusion = f32[256,32,128]{2,0,1:T(8,128)S(1)} fusion(f32[256,32,128]{2,0,1:T(8,128)S(1)} %copy-done.1, f32[256,32,128]{2,0,1:T(8,128)S(1)} %fusion.31, f32[256,32,128]{2,0,1:T(8,128)S(1)} %copy-done, f32[32,256,128]{2,1,0:T(8,128)S(1)} %bitcast.100, f32[256,32]{0,1:T(8,128)S(1)} %get-tuple-element.10, f32[256,32]{0,1:T(8,128)S(1)} %get-tuple-element.9), kind=kOutput, calls=%fused_computation.9 | convolution fusion | flops 3228434432 | bytes 21037056 | tf_op jit(solution)/shard_map/jb,kbc->jkc/dot_general | solution.py:87
  323.9 2.7 copy.25
  326.6 51.5 %all_to_all.86 = f32[256,32,128]{2,1,0:T(8,128)S(1)} all-to-all(f32[256,32,128]{2,1,0:T(8,128)S(1)} %copy.25), channel_id=1, replica_groups=mesh['gx'=8,'gy'=4] {'gx'}, dimensions={0} | all-to-all | bytes 8388608 | tf_op jit(solution)/shard_map/all_to_all | solution.py:93
  378.1 2.7 copy.26
  (23 shorter events, 2.2 us)
Async XLA Ops:
  121.4 30.4 %all-to-all-start.1 = ((f32[16,256,128]{2,0,1:T(8,128)}), f32[16,256,128]{2,0,1:T(8,128)S(1)}, u32[]{:S(2)}, u32[]{:S(2)}) async-start(f32[16,256,128]{2,0,1:T(8,128)} %copy.17), calls=%async_computation.1 | async-start | bytes 4194304 | tf_op jit(solution)/shard_map/all_to_all | solution.py:46
  151.8 31.5 %all-to-all-start.2 = ((f32[16,256,128]{2,0,1:T(8,128)}), f32[16,256,128]{2,0,1:T(8,128)}, u32[]{:S(2)}, u32[]{:S(2)}) async-start(f32[16,256,128]{2,0,1:T(8,128)} %rev.4), calls=%async_computation.2 | async-start | bytes 4194304 | tf_op jit(solution)/shard_map/all_to_all | solution.py:47
  183.3 2.8 copy-start.3
  191.1 2.2 copy-start.2
  256.5 53.7 %all-to-all-start.3 = ((f32[256,32,128]{2,1,0:T(8,128)}), f32[256,32,128]{2,1,0:T(8,128)}, u32[]{:S(2)}, u32[]{:S(2)}) async-start(f32[256,32,128]{2,1,0:T(8,128)} %get-tuple-element.5), calls=%async_computation.3 | async-start | bytes 8388608 | tf_op jit(solution)/shard_map/all_to_all | solution.py:77
  313.0 4.8 %copy-start = (f32[256,32,128]{2,0,1:T(8,128)S(1)}, f32[256,32,128]{2,0,1:T(8,128)}, u32[]{:S(2)}) copy-start(f32[256,32,128]{2,0,1:T(8,128)} %fusion.27) | copy-start | bytes 12582916
  313.0 4.8 %copy-start.1 = (f32[256,32,128]{2,0,1:T(8,128)S(1)}, f32[256,32,128]{2,0,1:T(8,128)}, u32[]{:S(2)}) copy-start(f32[256,32,128]{2,0,1:T(8,128)} %fusion.29) | copy-start | bytes 12582916
